TPU v7x, 32 devices: a whole 2x2x4 slice. The times are simulated.
32 devices in a mesh: groups: 2 (over x), blk: 8 (over z, y), rep: 2 (over core).
Axes of the slice: x: 2, y: 2, z: 4, core: 2. Of those that a mesh axis runs over, the one named last changes fastest.
Arguments:
- resident: bfloat16 [32768, 768], P(('groups', 'blk', 'rep')), parts along dimension 0, may hold values from -600 to 600
- ingest: bfloat16 [16384, 768], P(('groups', 'blk', 'rep')), parts along dimension 0, may hold values from -600 to 600
- cluster_ids: int32 [16384], P(('groups', 'blk', 'rep')), parts along dimension 0, may hold values from 0 to 127, as said below
Outputs:
- resident_score: float32 [32768], P(('groups', 'blk', 'rep')), parts along dimension 0
- ingest_score: float32 [16384], P(('groups', 'blk', 'rep')), parts along dimension 0
There are 2 independent parts, one for each index of `groups`. A program takes and returns all parts, laid end to end along the dimension named above; each array names one. Nothing has to cross between parts.
Inputs may be any that keep to these rules, and one draw needn't show every extreme that they name: `cluster_ids`: clusters 16 * p to 16 * p + 15 belong to cycle position p. At most 96 documents of one device belong to one cycle position, and in every draw some cycle position receives 96 from every device.
All inputs are finite; a program needn't handle non-finite values.
Results may differ from a plain program's by a relative error of at most 0.0003.
Values may be sent and summed in bfloat16 or wider, within the bound.
A program may use at most 64 MiB of HBM per device.

v0:
```python
import functools
import math

import jax
import jax.numpy as jnp
from jax import lax
from jax.experimental import pallas as pl
from jax.experimental.pallas import tpu as pltpu
from jax.sharding import PartitionSpec as P

INGEST_DEV = 512
CL_OWN = 16
CYCLE_STEPS = 4


temper = 0.2
epsilon = 1e-06


def shifted(value, axis, steps):
    count = lax.axis_size(axis)
    pairs = [(source, (source + steps) % count) for source in range(count)]
    return lax.ppermute(value, axis, pairs)


def unit_rows(rows):
    values = rows.astype(jnp.float32)
    squares = jnp.sum(values * values, axis=-1, keepdims=True) + epsilon
    factor = lax.rsqrt(squares)
    return (values * factor).astype(jnp.bfloat16)


def kernel_sums(visitors, occupancy, residents):
    count_rows = visitors.shape[0]
    block_rows = 512
    num_blocks = count_rows // block_rows
    visit_blocks = visitors.reshape(num_blocks, block_rows, visitors.shape[1])
    live_blocks = occupancy.astype(jnp.float32).reshape(num_blocks, block_rows)

    def tile_sums(running, pieces):
        visit_tile, live_tile = pieces
        scores = jnp.einsum("vd,rd->vr", visit_tile, residents, preferred_element_type=jnp.float32)
        kernel = jnp.exp((scores - 1.0) / temper)
        return (running + jnp.sum(kernel * live_tile[:, None], axis=0), jnp.sum(kernel, axis=1))

    resident_part, visit_parts = lax.scan(
        tile_sums, jnp.zeros((residents.shape[0],), jnp.float32), (visit_blocks, live_blocks)
    )
    return (visit_parts.reshape(count_rows), resident_part)


def on_device(resident, ingest, cluster_ids):
    cycle_size = lax.axis_size("blk")
    slot_count = 3 * INGEST_DEV // (2 * cycle_size)
    columns = ingest.shape[1]
    owners = cluster_ids // CL_OWN
    onehot = (owners[:, None] == jnp.arange(cycle_size, dtype=jnp.int32)[None, :]).astype(jnp.int32)
    rank_within = jnp.sum((jnp.cumsum(onehot, axis=0) - onehot) * onehot, axis=1)
    targets = owners * slot_count + rank_within
    unit_ingest = unit_rows(ingest)
    outgoing = (
        jnp.zeros((cycle_size * slot_count, columns), jnp.bfloat16).at[targets].set(unit_ingest)
    )
    filled = (
        jnp.zeros((cycle_size * slot_count,), jnp.bfloat16)
        .at[targets]
        .set(jnp.ones((ingest.shape[0],), jnp.bfloat16))
    )
    arrived, present = (
        lax.all_to_all(
            outgoing.reshape(cycle_size, slot_count, columns),
            "blk",
            split_axis=0,
            concat_axis=0,
            tiled=True,
        ),
        lax.all_to_all(
            filled.reshape(cycle_size, slot_count), "blk", split_axis=0, concat_axis=0, tiled=True
        ),
    )
    visitors, marked = (
        lax.all_gather(
            arrived.reshape(cycle_size * slot_count, columns), "rep", axis=0, tiled=True
        ),
        lax.all_gather(present.reshape(cycle_size * slot_count), "rep", axis=0, tiled=True),
    )
    unit_resident = unit_rows(resident)
    visit_total = jnp.zeros((visitors.shape[0],), jnp.float32)
    resident_total = jnp.zeros((resident.shape[0],), jnp.float32)
    moving = unit_resident
    for rotation in range(CYCLE_STEPS + 1):
        if rotation > 0:
            moving = shifted(moving, "blk", -1)
            resident_total = shifted(resident_total, "blk", -1)
        visit_part, resident_part = kernel_sums(visitors, marked, moving)
        visit_total = visit_total + visit_part
        resident_total = resident_total + resident_part
    resident_total = shifted(resident_total, "blk", CYCLE_STEPS)
    own_sums = lax.psum_scatter(visit_total, "rep", scatter_dimension=0, tiled=True)
    returned = lax.all_to_all(
        own_sums.reshape(cycle_size, slot_count), "blk", split_axis=0, concat_axis=0, tiled=True
    )
    density = returned.reshape(cycle_size * slot_count)[targets]
    return (jnp.log1p(resident_total), jnp.log1p(density))


PAIR = 2
LANES = 128
SUBLANES = 8
INGEST_CHUNK = 256
RESIDENT_CHUNK = 256
TILE = 1024
MESH = pl.DeviceIdType.MESH


def dense_kernel(
    cycle, ids_ref, ingest_ref, resident_ref, resident_out, ingest_out,
    raw_ingest, raw_resident, load_sem, rows, bank, ids, by_resident, by_ingest, resident_sums, ingest_sums, resident_terms, ingest_terms,
    up_send, down_send, rows_recv, ids_send, ids_recv, peer_send, peer_recv, core_send, core_recv,
    relay_send, relay_recv, part_send, part_recv, term_send, term_recv,
):
    line_size = cycle // PAIR
    me = lax.axis_index("blk")
    core = lax.axis_index("rep")
    line, side = me // PAIR, me % PAIR
    chunks = ingest_ref.shape[0] // INGEST_CHUNK
    held = resident_ref.shape[0]
    pieces = held // RESIDENT_CHUNK
    tiles = held // TILE
    steps = (line_size - 1) * chunks

    def device(at_line, at_side, at_core):
        return {"blk": at_line * PAIR + at_side, "rep": at_core}

    sibling = device(line, side, 1 - core)
    peer = device(line, 1 - side, core)
    across = device(line, 1 - side, 1 - core)

    def remote(source, target, send, recv, where):
        return pltpu.make_async_remote_copy(
            src_ref=source, dst_ref=target, send_sem=send, recv_sem=recv, device_id=where, device_id_type=MESH
        )

    def up_copy(c):
        return remote(rows.at[c], rows.at[c], up_send.at[c], rows_recv.at[c], device(line + 1, side, core))

    def down_copy(c):
        return remote(rows.at[c], rows.at[c], down_send.at[c], rows_recv.at[c], device(line - 1, side, core))

    def peer_copy(m):
        return remote(
            bank.at[pl.ds(m * RESIDENT_CHUNK, RESIDENT_CHUNK)],
            bank.at[pl.ds(2 * held + m * RESIDENT_CHUNK, RESIDENT_CHUNK)],
            peer_send.at[m], peer_recv.at[m], peer,
        )

    def relay_copy(m):
        return remote(
            bank.at[pl.ds(2 * held + m * RESIDENT_CHUNK, RESIDENT_CHUNK)],
            bank.at[pl.ds(3 * held + m * RESIDENT_CHUNK, RESIDENT_CHUNK)],
            relay_send.at[m], relay_recv.at[m], sibling,
        )

    core_copy = remote(bank.at[pl.ds(0, held)], bank.at[pl.ds(held, held)], core_send, core_recv, sibling)

    def ids_copy(other):
        mine = ids.at[pl.ds(line * chunks, chunks)]
        return remote(mine, mine, ids_send.at[other], ids_recv.at[line], device(other, side, core))

    def ids_arrival(other):
        theirs = ids.at[pl.ds(other * chunks, chunks)]
        return remote(theirs, theirs, ids_send.at[other], ids_recv.at[other], device(other, side, core))

    def term_copy(other):
        return remote(
            ingest_sums.at[pl.ds(other * chunks, chunks)], ingest_terms.at[pl.ds(line * chunks, chunks)],
            term_send.at[other], term_recv.at[line], device(other, side, core),
        )

    def term_arrival(other):
        return remote(
            ingest_sums.at[pl.ds(other * chunks, chunks)], ingest_terms.at[pl.ds(other * chunks, chunks)],
            term_send.at[other], term_recv.at[other], device(other, side, core),
        )

    def part_copy(slot):
        return remote(
            resident_sums.at[slot], resident_terms.at[slot], part_send.at[slot], part_recv.at[slot],
            (None, sibling, peer, across)[slot],
        )

    barrier = pltpu.get_barrier_semaphore()
    for where in (sibling, peer, across):
        pl.semaphore_signal(barrier, inc=1, device_id=where, device_id_type=MESH)
    for hop in range(1, line_size):
        pl.semaphore_signal(
            barrier, inc=1, device_id=device((line + hop) % line_size, side, core), device_id_type=MESH
        )

    ingest_load = pltpu.make_async_copy(ingest_ref, raw_ingest, load_sem.at[0])
    resident_load = pltpu.make_async_copy(resident_ref, raw_resident, load_sem.at[1])
    ids_load = pltpu.make_async_copy(ids_ref, ids.at[pl.ds(line * chunks, chunks)], load_sem.at[2])
    for load in (ingest_load, ids_load, resident_load):
        load.start()

    def unit(block):
        values = block.astype(jnp.float32)
        squares = jnp.sum(values * values, axis=-1, keepdims=True) + epsilon
        return (values * lax.rsqrt(squares)).astype(jnp.bfloat16)

    ingest_load.wait()
    for j in range(chunks):
        rows[line * chunks + j] = unit(raw_ingest[j * INGEST_CHUNK:(j + 1) * INGEST_CHUNK, :])
    ids_load.wait()
    pl.semaphore_wait(barrier, line_size + 2)
    for hop in range(1, line_size):
        ids_copy((line + hop) % line_size).start()
    for j in range(chunks):
        @pl.when(line + 1 < line_size)
        def _():
            up_copy(line * chunks + j).start()

        @pl.when(line > 0)
        def _():
            down_copy(line * chunks + j).start()

    resident_load.wait()

    @pl.loop(0, pieces)
    def _(m):
        part = pl.ds(m * RESIDENT_CHUNK, RESIDENT_CHUNK)
        bank[part, :] = unit(raw_resident[part, :])

    for m in range(pieces):
        peer_copy(m).start()
    core_copy.start()
    by_resident[...] = jnp.zeros_like(by_resident)
    by_ingest[...] = jnp.zeros_like(by_ingest)

    scale = math.log2(math.e) / temper
    span = CL_OWN * cycle

    def work(c, first, last):
        @pl.loop(first, last)
        def _(tile):
            part = pl.ds(tile * TILE, TILE)
            position = line * PAIR + jnp.where(tile < 2 * tiles, side, 1 - side)
            gap = (position + 1) * CL_OWN - 1 - ids[c]
            gap = jnp.where(gap < 0, gap + span, gap)
            bias = jnp.where(gap < CL_OWN * (CYCLE_STEPS + 1), -scale, -1e30)
            scores = lax.dot_general(
                bank[part, :], rows[c], (((1,), (1,)), ((), ())), preferred_element_type=jnp.float32
            )
            kernel = jnp.exp2(scores * scale + bias)
            by_ingest[c] += jnp.sum(kernel.reshape(TILE // SUBLANES, SUBLANES, INGEST_CHUNK), axis=0)
            folded = kernel[:, :LANES]
            for n in range(1, INGEST_CHUNK // LANES):
                folded = folded + kernel[:, n * LANES:(n + 1) * LANES]
            by_resident[part, :] += folded

    @pl.loop(0, 2)
    def _(half):
        @pl.when(half == 1)
        def _():
            core_copy.wait_recv()

        @pl.loop(0, chunks)
        def _(j):
            work(line * chunks + j, half * tiles, (half + 1) * tiles)

    for hop in range(1, line_size):
        ids_arrival((line + hop) % line_size).wait_recv()

    @pl.loop(0, steps)
    def _(step):
        hop, j = step // chunks + 1, step % chunks

        @pl.when(line - hop >= 0)
        def _():
            c = (line - hop) * chunks + j
            up_copy(c).wait_recv()

            @pl.when(line + 1 < line_size)
            def _():
                up_copy(c).start()

        @pl.when(line + hop < line_size)
        def _():
            c = (line + hop) * chunks + j
            down_copy(c).wait_recv()

            @pl.when(line > 0)
            def _():
                down_copy(c).start()

        @pl.when(step < pieces)
        def _():
            peer_copy(step).wait_recv()
            relay_copy(step).start()

        @pl.loop(0, 2)
        def _(way):
            other = line + (2 * way - 1) * hop

            @pl.when((other >= 0) & (other < line_size))
            def _():
                work(other * chunks + j, 0, jnp.where(step < pieces, 2 * tiles, 4 * tiles))

        @pl.when(step == pieces - 1)
        def _():
            for m in range(pieces):
                relay_copy(m).wait_recv()

            @pl.loop(0, line_size * chunks)
            def _(c):
                away = jnp.abs(c // chunks - line)
                arrived = (away - 1) * chunks + c % chunks

                @pl.when((away == 0) | (arrived < pieces))
                def _():
                    work(c, 2 * tiles, 4 * tiles)

    ingest_sums[...] = jnp.sum(by_ingest[...], axis=1, keepdims=True)

    def gather_slot(slot):
        block = by_resident[slot * held:(slot + 1) * held, :]
        resident_sums[slot] = jnp.sum(block.T, axis=0, keepdims=True)

    gather_slot(3)
    for hop in range(1, line_size):
        term_copy((line + hop) % line_size).start()
    gather_slot(2)
    part_copy(3).start()
    gather_slot(1)
    part_copy(2).start()
    gather_slot(0)
    part_copy(1).start()

    for c in range(line_size * chunks):
        @pl.when((c // chunks <= line) & (line + 1 < line_size))
        def _():
            up_copy(c).wait_send()

        @pl.when((c // chunks >= line) & (line > 0))
        def _():
            down_copy(c).wait_send()
    for m in range(pieces):
        peer_copy(m).wait_send()
        relay_copy(m).wait_send()
    core_copy.wait_send()

    resident_total = resident_sums[0]
    for slot in (1, 2, 3):
        part_copy(slot).wait()
        resident_total = resident_total + resident_terms[slot]
    resident_out[...] = resident_total
    ingest_total = ingest_sums[pl.ds(line * chunks, chunks)]
    for hop in range(1, line_size):
        other = (line + hop) % line_size
        term_arrival(other).wait_recv()
        ingest_total = ingest_total + ingest_terms[pl.ds(other * chunks, chunks)]
    ingest_out[...] = ingest_total
    for hop in range(1, line_size):
        other = (line + hop) % line_size
        ids_copy(other).wait_send()
        term_copy(other).wait_send()


def score_kernel(resident_total, ingest_total, resident_score, ingest_score):
    resident_score[...] = jnp.log1p(resident_total[...])
    ingest_score[...] = jnp.log1p(ingest_total[...])


def dense_on_device(cycle, resident, ingest, cluster_ids):
    held, columns = resident.shape
    count = ingest.shape[0]
    chunks = count // INGEST_CHUNK
    blocks = cycle // PAIR * chunks
    line_size = cycle // PAIR
    pieces = held // RESIDENT_CHUNK
    dma = pltpu.SemaphoreType.DMA
    vmem = pl.BlockSpec(memory_space=pltpu.VMEM)
    resident_total, ingest_total = pl.pallas_call(
        functools.partial(dense_kernel, cycle),
        out_shape=(
            jax.ShapeDtypeStruct((1, held), jnp.float32),
            jax.ShapeDtypeStruct((chunks, 1, INGEST_CHUNK), jnp.float32),
        ),
        in_specs=[pl.BlockSpec(memory_space=pl.ANY)] * 3,
        out_specs=(vmem, vmem),
        scratch_shapes=[
            pltpu.VMEM((count, columns), jnp.bfloat16),
            pltpu.VMEM((held, columns), jnp.bfloat16),
            dma((3,)),
            pltpu.VMEM((blocks, INGEST_CHUNK, columns), jnp.bfloat16),
            pltpu.VMEM((4 * held, columns), jnp.bfloat16),
            pltpu.VMEM((blocks, 1, INGEST_CHUNK), jnp.int32),
            pltpu.VMEM((4 * held, LANES), jnp.float32),
            pltpu.VMEM((blocks, SUBLANES, INGEST_CHUNK), jnp.float32),
            pltpu.VMEM((4, 1, held), jnp.float32),
            pltpu.VMEM((blocks, 1, INGEST_CHUNK), jnp.float32),
            pltpu.VMEM((4, 1, held), jnp.float32),
            pltpu.VMEM((blocks, 1, INGEST_CHUNK), jnp.float32),
            dma((blocks,)), dma((blocks,)), dma((blocks,)),
            dma((line_size,)), dma((line_size,)),
            dma((pieces,)), dma((pieces,)),
            dma, dma,
            dma((pieces,)), dma((pieces,)),
            dma((4,)), dma((4,)),
            dma((line_size,)), dma((line_size,)),
        ],
        compiler_params=pltpu.CompilerParams(collective_id=0, has_side_effects=True),
    )(cluster_ids.reshape(chunks, 1, INGEST_CHUNK), ingest, resident)
    resident_score, ingest_score = pl.pallas_call(
        score_kernel,
        out_shape=(
            jax.ShapeDtypeStruct(resident_total.shape, jnp.float32),
            jax.ShapeDtypeStruct(ingest_total.shape, jnp.float32),
        ),
        in_specs=[vmem] * 2,
        out_specs=(vmem, vmem),
    )(resident_total, ingest_total)
    return (resident_score.reshape(held), ingest_score.reshape(count))


def solution(mesh):
    in_specs = (
        P(("groups", "blk", "rep"), None),
        P(("groups", "blk", "rep"), None),
        P(("groups", "blk", "rep")),
    )
    out_specs = (P(("groups", "blk", "rep")), P(("groups", "blk", "rep")))
    cycle = mesh.shape["blk"]
    dense = 2 * (CYCLE_STEPS + 1) >= cycle and cycle % PAIR == 0 and mesh.shape["rep"] == 2
    body = functools.partial(dense_on_device, cycle) if dense else on_device
    return jax.shard_map(
        body, mesh=mesh, in_specs=in_specs, out_specs=out_specs, check_vma=False
    )
```

profile of v0, /device:TPU:0, one launch (start us, length us, event | category | flops | bytes accessed | tf_op | source)
XLA Modules:
  0.0 66.3 jit_solution(12814455104187836392)
XLA Ops:
  0.6 64.4 %shard_map.50 = (f32[1,1024]{1,0:T(1,128)}, f32[2,1,256]{2,1,0:T(1,128)}) custom-call(s32[2,1,256]{2,1,0:T(1,128)} %bitcast.3, bf16[512,768]{1,0:T(8,128)(2,1)} %ingest_ref.1, bf16[1024,768]{1,0:T(8,128)(2,1)} %resident_ref.1), custom_call_target="tpu_custom_call" | custom-call | tf_op jit(solution)/shard_map/pallas_call | solution.py:383
  65.1 1.3 %shard_map.51 = (f32[1,1024]{1,0:T(1,128)}, f32[2,1,256]{2,1,0:T(1,128)}) custom-call(f32[1,1024]{1,0:T(1,128)} %get-tuple-element.6.resident_total, f32[2,1,256]{2,1,0:T(1,128)} %get-tuple-element.7.ingest_total), custom_call_target="tpu_custom_call" | custom-call | tf_op jit(solution)/shard_map/pallas_call | solution.py:414
where the time goes:
time: 66.5 us; the launch traced here: 66.3 us
  Pallas kernels  65.7 us (99%)
    pallas_call x1, Pallas kernels, dense_on_device(): pl.pallas_call(functools.partial(dense_kernel, cycle), out_shape=(jax.Sha...  64.4 us

commit v1 on v0

--- a/solution.py
+++ b/solution.py
@@ -109,14 +109,14 @@
 SUBLANES = 8
 INGEST_CHUNK = 256
 RESIDENT_CHUNK = 256
-TILE = 1024
+HALVES = 2
 MESH = pl.DeviceIdType.MESH
 
 
 def dense_kernel(
     cycle, ids_ref, ingest_ref, resident_ref, resident_out, ingest_out,
     raw_ingest, raw_resident, load_sem, rows, bank, ids, by_resident, by_ingest, resident_sums, ingest_sums, resident_terms, ingest_terms,
-    up_send, down_send, rows_recv, ids_send, ids_recv, peer_send, peer_recv, core_send, core_recv,
+    up_send, down_send, rows_recv, up_ids_send, down_ids_send, ids_recv, peer_send, peer_recv, core_send, core_recv,
     relay_send, relay_recv, part_send, part_recv, term_send, term_recv,
 ):
     line_size = cycle // PAIR
@@ -126,8 +126,12 @@
     chunks = ingest_ref.shape[0] // INGEST_CHUNK
     held = resident_ref.shape[0]
     pieces = held // RESIDENT_CHUNK
-    tiles = held // TILE
+    tile_rows = 2 * held
     steps = (line_size - 1) * chunks
+    half_rows = INGEST_CHUNK // HALVES
+    at_end = (line == 0) | (line == line_size - 1)
+    below_end, above_end = line == 1, line == line_size - 2
+    holds_back = line_size > 2
 
     def device(at_line, at_side, at_core):
         return {"blk": at_line * PAIR + at_side, "rep": at_core}
@@ -141,11 +145,24 @@
             src_ref=source, dst_ref=target, send_sem=send, recv_sem=recv, device_id=where, device_id_type=MESH
         )
 
-    def up_copy(c):
-        return remote(rows.at[c], rows.at[c], up_send.at[c], rows_recv.at[c], device(line + 1, side, core))
-
-    def down_copy(c):
-        return remote(rows.at[c], rows.at[c], down_send.at[c], rows_recv.at[c], device(line - 1, side, core))
+    def row_copy(c, h, send, where):
+        part = rows.at[c, pl.ds(h * half_rows, half_rows)]
+        return remote(part, part, send.at[c, h], rows_recv.at[c, h], where)
+
+    def id_copy(c, send, where):
+        return remote(ids.at[c], ids.at[c], send.at[c], ids_recv.at[c], where)
+
+    above, below = device(line + 1, side, core), device(line - 1, side, core)
+
+    def up_copies(c):
+        return [id_copy(c, up_ids_send, above)] + [row_copy(c, h, up_send, above) for h in range(HALVES)]
+
+    def down_copies(c):
+        return [id_copy(c, down_ids_send, below)] + [row_copy(c, h, down_send, below) for h in range(HALVES)]
+
+    def start_all(copies):
+        for copy in copies:
+            copy.start()
 
     def peer_copy(m):
         return remote(
@@ -163,14 +180,6 @@
 
     core_copy = remote(bank.at[pl.ds(0, held)], bank.at[pl.ds(held, held)], core_send, core_recv, sibling)
 
-    def ids_copy(other):
-        mine = ids.at[pl.ds(line * chunks, chunks)]
-        return remote(mine, mine, ids_send.at[other], ids_recv.at[line], device(other, side, core))
-
-    def ids_arrival(other):
-        theirs = ids.at[pl.ds(other * chunks, chunks)]
-        return remote(theirs, theirs, ids_send.at[other], ids_recv.at[other], device(other, side, core))
-
     def term_copy(other):
         return remote(
             ingest_sums.at[pl.ds(other * chunks, chunks)], ingest_terms.at[pl.ds(line * chunks, chunks)],
@@ -192,10 +201,14 @@
     barrier = pltpu.get_barrier_semaphore()
     for where in (sibling, peer, across):
         pl.semaphore_signal(barrier, inc=1, device_id=where, device_id_type=MESH)
-    for hop in range(1, line_size):
-        pl.semaphore_signal(
-            barrier, inc=1, device_id=device((line + hop) % line_size, side, core), device_id_type=MESH
-        )
+
+    @pl.when(line > 0)
+    def _():
+        pl.semaphore_signal(barrier, inc=1, device_id=below, device_id_type=MESH)
+
+    @pl.when(line + 1 < line_size)
+    def _():
+        pl.semaphore_signal(barrier, inc=1, device_id=above, device_id_type=MESH)
 
     ingest_load = pltpu.make_async_copy(ingest_ref, raw_ingest, load_sem.at[0])
     resident_load = pltpu.make_async_copy(resident_ref, raw_resident, load_sem.at[1])
@@ -212,17 +225,17 @@
     for j in range(chunks):
         rows[line * chunks + j] = unit(raw_ingest[j * INGEST_CHUNK:(j + 1) * INGEST_CHUNK, :])
     ids_load.wait()
-    pl.semaphore_wait(barrier, line_size + 2)
-    for hop in range(1, line_size):
-        ids_copy((line + hop) % line_size).start()
+    pl.semaphore_wait(barrier, 3 + (line > 0).astype(jnp.int32) + (line + 1 < line_size).astype(jnp.int32))
     for j in range(chunks):
-        @pl.when(line + 1 < line_size)
-        def _():
-            up_copy(line * chunks + j).start()
-
-        @pl.when(line > 0)
-        def _():
-            down_copy(line * chunks + j).start()
+        kept = holds_back and j == chunks - 1
+
+        @pl.when((line + 1 < line_size) & jnp.logical_not(above_end & kept))
+        def _():
+            start_all(up_copies(line * chunks + j))
+
+        @pl.when((line > 0) & jnp.logical_not(below_end & kept))
+        def _():
+            start_all(down_copies(line * chunks + j))
 
     resident_load.wait()
 
@@ -243,8 +256,8 @@
     def work(c, first, last):
         @pl.loop(first, last)
         def _(tile):
-            part = pl.ds(tile * TILE, TILE)
-            position = line * PAIR + jnp.where(tile < 2 * tiles, side, 1 - side)
+            part = pl.ds(pl.multiple_of(tile * tile_rows, tile_rows), tile_rows)
+            position = line * PAIR + jnp.where(tile == 0, side, 1 - side)
             gap = (position + 1) * CL_OWN - 1 - ids[c]
             gap = jnp.where(gap < 0, gap + span, gap)
             bias = jnp.where(gap < CL_OWN * (CYCLE_STEPS + 1), -scale, -1e30)
@@ -252,46 +265,62 @@
                 bank[part, :], rows[c], (((1,), (1,)), ((), ())), preferred_element_type=jnp.float32
             )
             kernel = jnp.exp2(scores * scale + bias)
-            by_ingest[c] += jnp.sum(kernel.reshape(TILE // SUBLANES, SUBLANES, INGEST_CHUNK), axis=0)
+            by_ingest[c] += jnp.sum(kernel.reshape(tile_rows // SUBLANES, SUBLANES, INGEST_CHUNK), axis=0)
             folded = kernel[:, :LANES]
             for n in range(1, INGEST_CHUNK // LANES):
                 folded = folded + kernel[:, n * LANES:(n + 1) * LANES]
             by_resident[part, :] += folded
 
-    @pl.loop(0, 2)
-    def _(half):
-        @pl.when(half == 1)
-        def _():
-            core_copy.wait_recv()
-
-        @pl.loop(0, chunks)
-        def _(j):
-            work(line * chunks + j, half * tiles, (half + 1) * tiles)
-
-    for hop in range(1, line_size):
-        ids_arrival((line + hop) % line_size).wait_recv()
-
-    @pl.loop(0, steps)
-    def _(step):
-        hop, j = step // chunks + 1, step % chunks
+    core_copy.wait_recv()
+
+    @pl.loop(0, chunks)
+    def _(j):
+        work(line * chunks + j, 0, 1)
+
+    def place(step):
+        if not holds_back:
+            return step
+        turned = jnp.where(step == 0, 0, step + chunks - 1)
+        late = step >= steps - chunks + 1
+        return jnp.where(at_end & (chunks > 1), jnp.where(late, step - (steps - chunks), turned), step)
+
+    def rank(spot):
+        if not holds_back:
+            return spot
+        turned = jnp.where(spot == 0, 0, spot - chunks + 1)
+        late = (spot >= 1) & (spot < chunks)
+        return jnp.where(at_end & (chunks > 1), jnp.where(late, spot + steps - chunks, turned), spot)
+
+    def take(step):
+        spot = place(step)
+        hop, j = spot // chunks + 1, spot % chunks
 
         @pl.when(line - hop >= 0)
         def _():
-            c = (line - hop) * chunks + j
-            up_copy(c).wait_recv()
-
-            @pl.when(line + 1 < line_size)
+            for copy in up_copies((line - hop) * chunks + j):
+                copy.wait_recv()
+
+                @pl.when(line + 1 < line_size)
+                def _():
+                    copy.start()
+
+        @pl.when(line + hop < line_size)
+        def _():
+            for copy in down_copies((line + hop) * chunks + j):
+                copy.wait_recv()
+
+                @pl.when(line > 0)
+                def _():
+                    copy.start()
+
+        if holds_back:
+            @pl.when((step == (line_size - 2) * chunks - 1) & above_end)
             def _():
-                up_copy(c).start()
-
-        @pl.when(line + hop < line_size)
-        def _():
-            c = (line + hop) * chunks + j
-            down_copy(c).wait_recv()
-
-            @pl.when(line > 0)
+                start_all(up_copies(line * chunks + chunks - 1))
+
+            @pl.when((step == (line_size - 2) * chunks - 1) & below_end)
             def _():
-                down_copy(c).start()
+                start_all(down_copies(line * chunks + chunks - 1))
 
         @pl.when(step < pieces)
         def _():
@@ -304,7 +333,7 @@
 
             @pl.when((other >= 0) & (other < line_size))
             def _():
-                work(other * chunks + j, 0, jnp.where(step < pieces, 2 * tiles, 4 * tiles))
+                work(other * chunks + j, 0, jnp.where(step < pieces, 1, 2))
 
         @pl.when(step == pieces - 1)
         def _():
@@ -314,21 +343,42 @@
             @pl.loop(0, line_size * chunks)
             def _(c):
                 away = jnp.abs(c // chunks - line)
-                arrived = (away - 1) * chunks + c % chunks
+                arrived = rank((away - 1) * chunks + c % chunks)
 
                 @pl.when((away == 0) | (arrived < pieces))
                 def _():
-                    work(c, 2 * tiles, 4 * tiles)
-
-    ingest_sums[...] = jnp.sum(by_ingest[...], axis=1, keepdims=True)
+                    work(c, 1, 2)
+
+    @pl.loop(0, steps - 1)
+    def _(step):
+        take(step)
+
+    def return_terms(near):
+        for hop in range(1, line_size):
+            other = (line + hop) % line_size
+            away = jnp.abs(other - line)
+
+            @pl.when((away == 1) if near else (away > 1))
+            def _():
+                theirs = pl.ds(other * chunks, chunks)
+                ingest_sums[theirs] = jnp.sum(by_ingest[theirs], axis=1, keepdims=True)
+                term_copy(other).start()
+
+    early = pieces < steps
+    if early:
+        return_terms(False)
+    take(steps - 1)
+    if not early:
+        return_terms(False)
+    return_terms(True)
+    mine = pl.ds(line * chunks, chunks)
+    ingest_sums[mine] = jnp.sum(by_ingest[mine], axis=1, keepdims=True)
 
     def gather_slot(slot):
         block = by_resident[slot * held:(slot + 1) * held, :]
         resident_sums[slot] = jnp.sum(block.T, axis=0, keepdims=True)
 
     gather_slot(3)
-    for hop in range(1, line_size):
-        term_copy((line + hop) % line_size).start()
     gather_slot(2)
     part_copy(3).start()
     gather_slot(1)
@@ -339,11 +389,13 @@
     for c in range(line_size * chunks):
         @pl.when((c // chunks <= line) & (line + 1 < line_size))
         def _():
-            up_copy(c).wait_send()
+            for copy in up_copies(c):
+                copy.wait_send()
 
         @pl.when((c // chunks >= line) & (line > 0))
         def _():
-            down_copy(c).wait_send()
+            for copy in down_copies(c):
+                copy.wait_send()
     for m in range(pieces):
         peer_copy(m).wait_send()
         relay_copy(m).wait_send()
@@ -354,7 +406,7 @@
         part_copy(slot).wait()
         resident_total = resident_total + resident_terms[slot]
     resident_out[...] = resident_total
-    ingest_total = ingest_sums[pl.ds(line * chunks, chunks)]
+    ingest_total = ingest_sums[mine]
     for hop in range(1, line_size):
         other = (line + hop) % line_size
         term_arrival(other).wait_recv()
@@ -362,7 +414,6 @@
     ingest_out[...] = ingest_total
     for hop in range(1, line_size):
         other = (line + hop) % line_size
-        ids_copy(other).wait_send()
         term_copy(other).wait_send()
 
 
@@ -401,8 +452,8 @@
             pltpu.VMEM((blocks, 1, INGEST_CHUNK), jnp.float32),
             pltpu.VMEM((4, 1, held), jnp.float32),
             pltpu.VMEM((blocks, 1, INGEST_CHUNK), jnp.float32),
+            dma((blocks, HALVES)), dma((blocks, HALVES)), dma((blocks, HALVES)),
             dma((blocks,)), dma((blocks,)), dma((blocks,)),
-            dma((line_size,)), dma((line_size,)),
             dma((pieces,)), dma((pieces,)),
             dma, dma,
             dma((pieces,)), dma((pieces,)),

time: 66.5 us -> 65.9 us (level)
  no operation moved by 1% of the time
where the time goes in v1:
time: 65.9 us; the launch traced here: 65.7 us
  Pallas kernels  65.1 us (99%)
    pallas_call x1, Pallas kernels, dense_on_device(): pl.pallas_call(functools.partial(dense_kernel, cycle), out_shape=(jax.Sha...  63.8 us

profile of v1, /device:TPU:0, one launch (start us, length us, event | category | flops | bytes accessed | tf_op | source)
XLA Modules:
  0.0 65.7 jit_solution(16570400865292362584)
XLA Ops:
  0.6 63.8 %shard_map.50 = (f32[1,1024]{1,0:T(1,128)}, f32[2,1,256]{2,1,0:T(1,128)}) custom-call(s32[2,1,256]{2,1,0:T(1,128)} %bitcast.3, bf16[512,768]{1,0:T(8,128)(2,1)} %ingest_ref.1, bf16[1024,768]{1,0:T(8,128)(2,1)} %resident_ref.1), custom_call_target="tpu_custom_call" | custom-call | tf_op jit(solution)/shard_map/pallas_call | solution.py:434
  64.4 1.3 %shard_map.51 = (f32[1,1024]{1,0:T(1,128)}, f32[2,1,256]{2,1,0:T(1,128)}) custom-call(f32[1,1024]{1,0:T(1,128)} %get-tuple-element.6.resident_total, f32[2,1,256]{2,1,0:T(1,128)} %get-tuple-element.7.ingest_total), custom_call_target="tpu_custom_call" | custom-call | tf_op jit(solution)/shard_map/pallas_call | solution.py:465

commit v2 on v1

--- a/solution.py
+++ b/solution.py
@@ -110,6 +110,8 @@
 INGEST_CHUNK = 256
 RESIDENT_CHUNK = 256
 HALVES = 2
+LINE = 4
+SUBS = 8
 MESH = pl.DeviceIdType.MESH
 
 
@@ -420,6 +422,20 @@
 def score_kernel(resident_total, ingest_total, resident_score, ingest_score):
     resident_score[...] = jnp.log1p(resident_total[...])
     ingest_score[...] = jnp.log1p(ingest_total[...])
+
+
+def scores_of(resident_total, ingest_total, held, count):
+    vmem = pl.BlockSpec(memory_space=pltpu.VMEM)
+    resident_score, ingest_score = pl.pallas_call(
+        score_kernel,
+        out_shape=(
+            jax.ShapeDtypeStruct(resident_total.shape, jnp.float32),
+            jax.ShapeDtypeStruct(ingest_total.shape, jnp.float32),
+        ),
+        in_specs=[vmem] * 2,
+        out_specs=(vmem, vmem),
+    )(resident_total, ingest_total)
+    return (resident_score.reshape(held), ingest_score.reshape(count))
 
 
 def dense_on_device(cycle, resident, ingest, cluster_ids):
@@ -462,16 +478,630 @@
         ],
         compiler_params=pltpu.CompilerParams(collective_id=0, has_side_effects=True),
     )(cluster_ids.reshape(chunks, 1, INGEST_CHUNK), ingest, resident)
-    resident_score, ingest_score = pl.pallas_call(
-        score_kernel,
+    return scores_of(resident_total, ingest_total, held, count)
+
+
+def relay_kernel(
+    cycle, ids_ref, ingest_ref, resident_ref, resident_out, ingest_out,
+    raw_ingest, raw_resident, rows, guest, bank, ids, by_resident, by_ingest, resident_sums, ingest_sums,
+    resident_terms, ingest_terms,
+    load_sem, up_send, down_send, rows_recv, up_ids_send, down_ids_send, ids_recv,
+    guest_send, guest_recv, guest_pass, out_send, out_recv, out_pass, direct_send, far_recv,
+    peer_send, peer_recv, turn_send, turn_recv, turn_pass, cross_send, core_send, core_recv,
+    near_send, near_recv, away_send, away_recv, part_send, part_recv, term_send, term_recv,
+):
+    group = lax.axis_index("groups")
+    me = lax.axis_index("blk")
+    core = lax.axis_index("rep")
+    level, side = me // PAIR, me % PAIR
+    role = jnp.where(group == 0, level, LINE - 1 - level)
+    count, held = ingest_ref.shape[0], resident_ref.shape[0]
+    chunk, half = count // 2, count // 4
+    sub = held // SUBS
+    quad = held // 2
+
+    def level_of(at_role, at_group):
+        return jnp.where(at_group == 0, at_role, LINE - 1 - at_role)
+
+    def device(at_role, at_side, at_core):
+        return {"groups": group, "blk": level_of(at_role, group) * PAIR + at_side, "rep": at_core}
+
+    def other(at_role, at_side):
+        return {"groups": 1 - group, "blk": level_of(at_role, 1 - group) * PAIR + at_side, "rep": core}
+
+    sibling = device(role, side, 1 - core)
+    peer = device(role, 1 - side, core)
+    across = device(role, 1 - side, 1 - core)
+    above, below = device(role + 1, side, core), device(role - 1, side, core)
+
+    def remote(source, target, send, recv, where):
+        return pltpu.make_async_remote_copy(
+            src_ref=source, dst_ref=target, send_sem=send, recv_sem=recv, device_id=where, device_id_type=MESH
+        )
+
+    def got(target, recv):
+        remote(target, target, core_send, recv, sibling).wait_recv()
+
+    def part(c, h):
+        return rows.at[pl.ds(c * chunk + h * half, half)]
+
+    def strip(start, size):
+        return bank.at[pl.ds(start, size)]
+
+    def own_at(r):
+        return r * sub
+
+    def peer_at(r, theirs=0):
+        return 2 * held + (r // 4) * held + (r % 4) * sub + theirs * quad
+
+    def far_at(line, r, theirs=0):
+        if line == 0:
+            return 4 * held + (r // 4) * held + (r % 4) * sub + theirs * quad
+        if r < 4:
+            return 6 * held + r * sub + theirs * quad
+        return 7 * held + (r - 4) // 2 * quad + (r % 2) * sub + theirs * (quad // 2)
+
+    def up(c, h):
+        return remote(part(c, h), part(c, h), up_send.at[c, h], rows_recv.at[c, h], above)
+
+    def down(c, h):
+        return remote(part(c, h), part(c, h), down_send.at[c, h], rows_recv.at[c, h], below)
+
+    def up_ids(c):
+        return remote(ids.at[c], ids.at[c], up_ids_send.at[c], ids_recv.at[c], above)
+
+    def down_ids(c):
+        return remote(ids.at[c], ids.at[c], down_ids_send.at[c], ids_recv.at[c], below)
+
+    def guest_part(h):
+        return guest.at[pl.ds(h * half, half)]
+
+    def guest_copy(h):
+        return remote(part(3, h), guest_part(h), guest_send.at[h], guest_recv.at[h], other(2, side))
+
+    def guest_on(h):
+        return remote(guest_part(h), part(3, h), guest_pass.at[h], rows_recv.at[3, h], other(0, side))
+
+    def out_spot(i):
+        return (0, i) if i < 4 else (1, i - 4)
+
+    def out_copy(i):
+        line, r = out_spot(i)
+        source = own_at(r) if line == 0 else peer_at(r)
+        return remote(
+            strip(source, sub), strip(far_at(line, r), sub), out_send.at[i], out_recv.at[i], other(0, side)
+        )
+
+    def out_on(i):
+        line, r = out_spot(i)
+        spot = strip(far_at(line, r), sub)
+        return remote(spot, spot, out_pass.at[i], far_recv.at[line, r], other(2, side))
+
+    def direct_copy(i):
+        line, r = (0, i + 4) if i < 4 else (1, i - 2)
+        source = own_at(r) if line == 0 else peer_at(r)
+        return remote(
+            strip(source, sub), strip(far_at(line, r), sub), direct_send.at[i], far_recv.at[line, r], below
+        )
+
+    def peer_copy(r):
+        return remote(strip(own_at(r), sub), strip(peer_at(r), sub), peer_send.at[r], peer_recv.at[r], peer)
+
+    def turn_copy(k):
+        r = k + 6
+        return remote(
+            strip(own_at(r), sub), strip(far_at(0, r), sub), turn_send.at[k], turn_recv.at[k], other(1, 1 - side)
+        )
+
+    def turn_on(k):
+        r = k + 6
+        return remote(
+            strip(far_at(0, r), sub), strip(peer_at(r), sub), turn_pass.at[k], peer_recv.at[r], other(2, side)
+        )
+
+    def cross_copy(r):
+        return remote(
+            strip(far_at(0, r), sub), strip(far_at(1, r), sub), cross_send.at[r - 4], far_recv.at[1, r], peer
+        )
+
+    core_copy = remote(strip(0, held), strip(held, held), core_send, core_recv, sibling)
+
+    def near_copy(r):
+        return remote(strip(peer_at(r), sub), strip(peer_at(r, 1), sub), near_send.at[r], near_recv.at[r], sibling)
+
+    def away_copy(line, r):
+        return remote(
+            strip(far_at(line, r), sub), strip(far_at(line, r, 1), sub),
+            away_send.at[line, r], away_recv.at[line, r], sibling,
+        )
+
+    def term_copy(k):
+        return remote(
+            ingest_sums.at[pl.ds(2 * k, 2)], ingest_terms.at[role], term_send.at[k], term_recv.at[role],
+            device(k, side, core),
+        )
+
+    def term_got(k):
+        got(ingest_terms.at[k], term_recv.at[k])
+
+    def part_copy(slot):
+        if slot >= 4:
+            where = device(3, side if slot < 6 else 1 - side, core if slot % 2 == 0 else 1 - core)
+        else:
+            where = (None, sibling, peer, across)[slot]
+        return remote(resident_sums.at[slot], resident_terms.at[slot], part_send.at[slot], part_recv.at[slot], where)
+
+    inner = (role == 1) | (role == 2)
+    barrier = pltpu.get_barrier_semaphore()
+
+    def greet(where):
+        pl.semaphore_signal(barrier, inc=1, device_id=where, device_id_type=MESH)
+
+    for where in (sibling, peer, across, other(LINE - 1 - role, side)):
+        greet(where)
+    pl.when(role > 0)(lambda: greet(below))
+    pl.when(role < LINE - 1)(lambda: greet(above))
+    pl.when(inner)(lambda: greet(other(LINE - 1 - role, 1 - side)))
+    greeted = (
+        4 + (role > 0).astype(jnp.int32) + (role < LINE - 1).astype(jnp.int32) + inner.astype(jnp.int32)
+    )
+
+    def ingest_load(s):
+        piece = pl.ds(s * half, half)
+        return pltpu.make_async_copy(ingest_ref.at[piece], raw_ingest.at[piece], load_sem.at[s])
+
+    def resident_load(m):
+        piece = pl.ds(m * 2 * sub, 2 * sub)
+        return pltpu.make_async_copy(resident_ref.at[piece], raw_resident.at[piece], load_sem.at[4 + m])
+
+    ids_load = pltpu.make_async_copy(ids_ref, ids.at[pl.ds(2 * role, 2)], load_sem.at[8])
+    ingest_load(0).start()
+    ids_load.start()
+    for s in range(1, 4):
+        ingest_load(s).start()
+    for m in range(4):
+        resident_load(m).start()
+
+    def unit(block):
+        values = block.astype(jnp.float32)
+        squares = jnp.sum(values * values, axis=-1, keepdims=True) + epsilon
+        return (values * lax.rsqrt(squares)).astype(jnp.bfloat16)
+
+    def ready(s):
+        ingest_load(s).wait()
+        rows[pl.ds(role * count + s * half, half), :] = unit(raw_ingest[s * half:(s + 1) * half, :])
+
+    ready(0)
+    ids_load.wait()
+    pl.semaphore_wait(barrier, greeted)
+    for s in range(4):
+        j, h = s // 2, s % 2
+        if s:
+            ready(s)
+        c = 2 * role + j
+
+        @pl.when((role == 1) | (role == 2) | ((role == 0) & (j == 0)))
+        def _():
+            up(c, h).start()
+
+        @pl.when((role == 2) | ((role == 1) & (j == 0)) | ((role == 3) & (j == 0)))
+        def _():
+            down(c, h).start()
+
+        if j == 1:
+            @pl.when(role == 1)
+            def _():
+                guest_copy(h).start()
+        if s == 0:
+            for k in range(2):
+                @pl.when(role < 3)
+                def _():
+                    up_ids(2 * role + k).start()
+
+                @pl.when(role > 0)
+                def _():
+                    down_ids(2 * role + k).start()
+
+    for m in range(4):
+        resident_load(m).wait()
+        piece = pl.ds(m * 2 * sub, 2 * sub)
+        bank[piece, :] = unit(raw_resident[piece, :])
+        for r in (2 * m, 2 * m + 1):
+            @pl.when((role < 2) | ((role == 2) & (r < 6)) | ((role == 3) & (r < 4)))
+            def _():
+                peer_copy(r).start()
+
+            if r >= 6:
+                @pl.when(role == 2)
+                def _():
+                    turn_copy(r - 6).start()
+
+            if r < 4:
+                @pl.when(role == 3)
+                def _():
+                    out_copy(r).start()
+            else:
+                @pl.when(role == 3)
+                def _():
+                    direct_copy(r - 4).start()
+            if r == 5:
+                @pl.when(role == 3)
+                def _():
+                    down(7, 0).start()
+                    down(7, 1).start()
+    core_copy.start()
+    by_resident[pl.ds(0, 4 * held), :] = jnp.zeros((4 * held, LANES), jnp.float32)
+    by_ingest[...] = jnp.zeros_like(by_ingest)
+
+    @pl.when(role == 2)
+    def _():
+        by_resident[pl.ds(4 * held, 4 * held), :] = jnp.zeros((4 * held, LANES), jnp.float32)
+
+    scale = math.log2(math.e) / temper
+    span = CL_OWN * cycle
+
+    def work(c, start, size, position):
+        spot = pl.ds(start, size)
+        gap = (position + 1) * CL_OWN - 1 - ids[c]
+        gap = jnp.where(gap < 0, gap + span, gap)
+        bias = jnp.where(gap < CL_OWN * (CYCLE_STEPS + 1), -scale, -1e30)
+        block = rows[pl.ds(pl.multiple_of(c * chunk, chunk), chunk), :]
+        scores = lax.dot_general(bank[spot, :], block, (((1,), (1,)), ((), ())), preferred_element_type=jnp.float32)
+        kernel = jnp.exp2(scores * scale + bias)
+        by_ingest[c] += jnp.sum(kernel.reshape(size // SUBLANES, SUBLANES, chunk), axis=0)
+        folded = kernel[:, :LANES]
+        for n in range(1, chunk // LANES):
+            folded = folded + kernel[:, n * LANES:(n + 1) * LANES]
+        by_resident[spot, :] += folded
+
+    here = level * PAIR + side
+    beside = level * PAIR + 1 - side
+    end = level_of(3, group) * PAIR
+    home = (0, 2 * held, here)
+    next0 = (2 * held, held, beside)
+    next1 = (3 * held, held, beside)
+    next_all = (2 * held, 2 * held, beside)
+    far_all = (4 * held, 2 * held, end + side)
+    far2 = (6 * held, held, end + 1 - side)
+    far3 = (7 * held, quad, end + 1 - side)
+    far4 = (7 * held + quad, quad, end + 1 - side)
+
+    def do(first, last, *blocks):
+        @pl.loop(first, last)
+        def _(c):
+            for block in blocks:
+                work(c, *block)
+
+    def take(c, h, *onward):
+        got(part(c, h), rows_recv.at[c, h])
+        if h == 0:
+            got(ids.at[c], ids_recv.at[c])
+        for way in onward:
+            way(c, h).start()
+            if h == 0:
+                (up_ids if way is up else down_ids)(c).start()
+
+    def meet(*subs):
+        for r in subs:
+            got(strip(peer_at(r), sub), peer_recv.at[r])
+            near_copy(r).start()
+
+    def met(*subs):
+        for r in subs:
+            got(strip(peer_at(r, 1), sub), near_recv.at[r])
+
+    def reach(line, *subs):
+        for r in subs:
+            got(strip(far_at(line, r), sub), far_recv.at[line, r])
+            if line == 0 and r >= 4:
+                cross_copy(r).start()
+            away_copy(line, r).start()
+
+    def reached(line, *subs):
+        for r in subs:
+            got(strip(far_at(line, r, 1), sub), away_recv.at[line, r])
+
+    def pass_out(i):
+        line, r = out_spot(i)
+        got(strip(far_at(line, r), sub), out_recv.at[i])
+        out_on(i).start()
+
+    core_copy.wait_recv()
+
+    @pl.loop(0, 2)
+    def _(j):
+        work(2 * role + j, *home)
+
+    @pl.when(role == 0)
+    def _():
+        pass_out(0)
+        pass_out(1)
+        up(1, 0).start()
+        up(1, 1).start()
+        take(2, 0)
+        take(2, 1)
+        meet(0, 1)
+        do(2, 3, home)
+        take(3, 0)
+        take(3, 1)
+        take(4, 0)
+        pass_out(2)
+        meet(2)
+        take(4, 1)
+        pass_out(3)
+        meet(3)
+        do(3, 5, home)
+        met(0, 1, 2, 3)
+        do(0, 5, next0)
+        take(5, 0)
+        meet(4)
+        pass_out(4)
+        take(5, 1)
+        meet(5)
+        pass_out(5)
+        do(5, 6, home, next0)
+        take(6, 0)
+        meet(6)
+        take(6, 1)
+        meet(7)
+        do(6, 7, home, next0)
+        met(4, 5, 6, 7)
+        do(0, 7, next1)
+        take(7, 0)
+        take(7, 1)
+        do(7, 8, home, next_all)
+
+    @pl.when(role == 1)
+    def _():
+        take(0, 0, up)
+        take(4, 0, down)
+        take(0, 1, up)
+        take(4, 1, down)
+        meet(0)
+        do(0, 1, home)
+        do(4, 5, home)
+        take(5, 0, down)
+        meet(1)
+        take(5, 1, down)
+        do(5, 6, home)
+        for k in range(2):
+            got(strip(far_at(0, k + 6), sub), turn_recv.at[k])
+            turn_on(k).start()
+        meet(2)
+        take(1, 0, up)
+        take(6, 0, down)
+        meet(3)
+        take(1, 1, up)
+        take(6, 1, down)
+        do(1, 2, home)
+        do(6, 7, home)
+        met(0, 1, 2, 3)
+        do(0, 4, next0)
+        take(7, 0, down)
+        meet(4)
+        do(4, 7, next0)
+        take(7, 1, down)
+        meet(5)
+        do(7, 8, home, next0)
+        meet(6, 7)
+        met(4, 5, 6, 7)
+        do(0, 8, next1)
+
+    @pl.when(role == 2)
+    def _():
+        take(6, 0, down)
+        for h in range(2):
+            got(guest_part(h), guest_recv.at[h])
+            guest_on(h).start()
+            if h == 0:
+                take(2, 0, up)
+                take(6, 1, down)
+        take(2, 1, up)
+        meet(0, 1)
+        do(2, 3, home)
+        do(6, 7, home)
+        take(3, 0, up)
+        reach(0, 4)
+        meet(2)
+        take(3, 1, up)
+        reach(0, 5)
+        meet(3)
+        do(3, 4, home)
+        reach(0, 0, 1)
+        met(0, 1, 2, 3)
+        do(2, 5, next0)
+        take(7, 0, down)
+        do(5, 7, next0)
+        take(7, 1, down)
+        do(7, 8, home, next0)
+        take(0, 0)
+        take(0, 1)
+        meet(4, 5, 6, 7)
+        do(0, 1, home, next0)
+        met(4, 5, 6, 7)
+        do(2, 5, next1)
+        reach(0, 6)
+        do(5, 8, next1)
+        take(1, 0)
+        take(1, 1)
+        do(0, 1, next1)
+        reach(0, 7)
+        do(1, 2, home, next_all)
+        reach(1, 4, 5)
+        reach(0, 2, 3)
+        reached(0, 0, 1, 2, 3, 4, 5, 6, 7)
+        do(0, 2, far_all)
+        reached(1, 4, 5)
+        do(0, 8, far3)
+        reach(1, 2, 6, 0, 3, 7, 1)
+        reached(1, 6, 7)
+        do(0, 8, far4)
+        reached(1, 0, 1, 2, 3)
+        do(0, 2, far2)
+
+    @pl.when(role == 3)
+    def _():
+        for r in range(2):
+            meet(r)
+            out_copy(4 + r).start()
+        take(4, 0)
+        take(4, 1)
+        do(4, 5, home)
+        for r in range(2, 4):
+            meet(r)
+            direct_copy(r + 2).start()
+        met(0, 1, 2, 3)
+        do(6, 8, next0)
+        do(4, 5, next0)
+        take(5, 0)
+        take(5, 1)
+        do(5, 6, home, next0)
+        take(2, 0)
+        take(2, 1)
+        do(2, 3, home, next0)
+        take(3, 0)
+        take(3, 1)
+        do(3, 4, home, next0)
+
+    ingest_sums[...] = jnp.sum(by_ingest[...], axis=1, keepdims=True)
+    for k in range(LINE):
+        @pl.when((role != k) & ((role < 3) | (k > 0)))
+        def _():
+            term_copy(k).start()
+
+    def gather(start, size):
+        return jnp.sum(by_resident[start:start + size, :].T, axis=0, keepdims=True)
+
+    def gather_pair(slot, first, second):
+        resident_sums[slot, :, 0:quad] = gather(first, quad)
+        resident_sums[slot, :, quad:held] = gather(second, quad)
+        part_copy(slot).start()
+
+    @pl.when(role == 2)
+    def _():
+        for slot in (6, 7):
+            resident_sums[slot, :, 0:quad] = gather(far_at(1, 0, slot % 2), quad)
+            for n in range(2):
+                resident_sums[slot, :, quad + n * quad // 2:quad + (n + 1) * quad // 2] = gather(
+                    far_at(1, 4 + 2 * n, slot % 2), quad // 2
+                )
+            part_copy(slot).start()
+        for slot in (4, 5):
+            gather_pair(slot, far_at(0, 0, slot % 2), far_at(0, 4, slot % 2))
+
+    gather_pair(3, peer_at(0, 1), peer_at(4, 1))
+    gather_pair(2, peer_at(0), peer_at(4))
+    resident_sums[1] = gather(held, held)
+    part_copy(1).start()
+    resident_total = gather(0, held)
+
+    for slot in (1, 2, 3):
+        got(resident_terms.at[slot], part_recv.at[slot])
+        resident_total = resident_total + resident_terms[slot]
+    resident_out[...] = resident_total
+
+    @pl.when(role == 3)
+    def _():
+        far_total = resident_out[...]
+        for slot in (4, 5, 6, 7):
+            got(resident_terms.at[slot], part_recv.at[slot])
+            far_total = far_total + resident_terms[slot]
+        resident_out[...] = far_total
+
+    ingest_out[...] = ingest_sums[pl.ds(2 * role, 2)]
+    for k in range(LINE):
+        @pl.when((role != k) & ((k < 3) | (role > 0)))
+        def _():
+            term_got(k)
+            ingest_out[...] += ingest_terms[k]
+
+    for k in range(LINE):
+        @pl.when((role != k) & ((role < 3) | (k > 0)))
+        def _():
+            term_copy(k).wait_send()
+    for slot in (1, 2, 3):
+        part_copy(slot).wait_send()
+    core_copy.wait_send()
+
+    def sent(condition, *copies):
+        @pl.when(condition)
+        def _():
+            for copy in copies:
+                copy().wait_send()
+
+    def later(make, *arguments):
+        return lambda: make(*arguments)
+
+    pairs = [(c, h) for c in range(8) for h in range(2)]
+
+    def flows(make, make_ids, chunks):
+        return [later(make, c, h) for c, h in pairs if c in chunks] + [later(make_ids, c) for c in chunks]
+
+    sent(
+        role == 0,
+        *flows(up, up_ids, (0, 1)), *[later(out_on, i) for i in range(6)],
+        *[later(peer_copy, r) for r in range(8)], *[later(near_copy, r) for r in range(8)],
+    )
+    sent(
+        role == 1,
+        *flows(up, up_ids, (0, 1, 2, 3)), *flows(down, down_ids, (2, 4, 5, 6, 7)), later(down_ids, 3),
+        *[later(guest_copy, h) for h in range(2)], *[later(turn_on, k) for k in range(2)],
+        *[later(peer_copy, r) for r in range(8)], *[later(near_copy, r) for r in range(8)],
+    )
+    sent(
+        role == 2,
+        *flows(up, up_ids, (2, 3, 4, 5)), *flows(down, down_ids, (4, 5, 6, 7)),
+        *[later(guest_on, h) for h in range(2)], *[later(turn_copy, k) for k in range(2)],
+        *[later(peer_copy, r) for r in range(6)], *[later(near_copy, r) for r in range(8)],
+        *[later(cross_copy, r) for r in range(4, 8)],
+        *[later(away_copy, line, r) for line in range(2) for r in range(8)],
+        *[later(part_copy, slot) for slot in (4, 5, 6, 7)],
+    )
+    sent(
+        role == 3,
+        *flows(down, down_ids, (6, 7)), *[later(out_copy, i) for i in range(6)],
+        *[later(direct_copy, i) for i in range(6)],
+        *[later(peer_copy, r) for r in range(4)], *[later(near_copy, r) for r in range(4)],
+    )
+
+
+def relay_on_device(cycle, resident, ingest, cluster_ids):
+    held, columns = resident.shape
+    count = ingest.shape[0]
+    chunk = count // 2
+    dma = pltpu.SemaphoreType.DMA
+    vmem = pl.BlockSpec(memory_space=pltpu.VMEM)
+    flows = dma((8, 2))
+    eight = dma((8,))
+    totals = pl.pallas_call(
+        functools.partial(relay_kernel, cycle),
         out_shape=(
-            jax.ShapeDtypeStruct(resident_total.shape, jnp.float32),
-            jax.ShapeDtypeStruct(ingest_total.shape, jnp.float32),
+            jax.ShapeDtypeStruct((1, held), jnp.float32),
+            jax.ShapeDtypeStruct((2, 1, chunk), jnp.float32),
         ),
-        in_specs=[vmem] * 2,
+        in_specs=[pl.BlockSpec(memory_space=pl.ANY)] * 3,
         out_specs=(vmem, vmem),
-    )(resident_total, ingest_total)
-    return (resident_score.reshape(held), ingest_score.reshape(count))
+        scratch_shapes=[
+            pltpu.VMEM((count, columns), jnp.bfloat16),
+            pltpu.VMEM((held, columns), jnp.bfloat16),
+            pltpu.VMEM((LINE * count, columns), jnp.bfloat16),
+            pltpu.VMEM((chunk, columns), jnp.bfloat16),
+            pltpu.VMEM((8 * held, columns), jnp.bfloat16),
+            pltpu.VMEM((2 * LINE, 1, chunk), jnp.int32),
+            pltpu.VMEM((8 * held, LANES), jnp.float32),
+            pltpu.VMEM((2 * LINE, SUBLANES, chunk), jnp.float32),
+            pltpu.VMEM((8, 1, held), jnp.float32),
+            pltpu.VMEM((2 * LINE, 1, chunk), jnp.float32),
+            pltpu.VMEM((8, 1, held), jnp.float32),
+            pltpu.VMEM((LINE, 2, 1, chunk), jnp.float32),
+            dma((9,)), flows, flows, flows, eight, eight, eight,
+            dma((2,)), dma((2,)), dma((2,)), dma((6,)), dma((6,)), dma((6,)), dma((6,)), dma((2, 8)),
+            eight, eight, dma((2,)), dma((2,)), dma((2,)), dma((4,)), dma, dma,
+            eight, eight, dma((2, 8)), dma((2, 8)), eight, eight, dma((LINE,)), dma((LINE,)),
+        ],
+        compiler_params=pltpu.CompilerParams(collective_id=0, has_side_effects=True),
+    )(cluster_ids.reshape(2, 1, chunk), ingest, resident)
+    return scores_of(*totals, held, count)
 
 
 def solution(mesh):
@@ -484,6 +1114,8 @@
     cycle = mesh.shape["blk"]
     dense = 2 * (CYCLE_STEPS + 1) >= cycle and cycle % PAIR == 0 and mesh.shape["rep"] == 2
     body = functools.partial(dense_on_device, cycle) if dense else on_device
+    if dense and cycle == LINE * PAIR and mesh.shape["groups"] == 2:
+        body = functools.partial(relay_on_device, cycle)
     return jax.shard_map(
         body, mesh=mesh, in_specs=in_specs, out_specs=out_specs, check_vma=False
     )

time: 65.9 us -> 85.7 us (1.30); the launches traced: 65.7 us -> 86.6 us
  Pallas kernels: 65.1 us -> 85.6 us
    pallas_call x2, Pallas kernels: 65.1 us -> 85.6 us  [the longest x1 84.3 us: relay_on_device(): pl.pallas_call(functools.partial(relay_kernel, cycle), out_shape=(jax.Sha...]
where the time goes in v2:
time: 85.7 us; the launch traced here: 86.6 us
  Pallas kernels  85.6 us (100%)
  between operations  1.02 us (1%)
    pallas_call x1, Pallas kernels, relay_on_device(): pl.pallas_call(functools.partial(relay_kernel, cycle), out_shape=(jax.Sha...  84.3 us

profile of v2, /device:TPU:0, one launch (start us, length us, event | category | flops | bytes accessed | tf_op | source)
XLA Modules:
  0.0 86.6 jit_solution(18296881203117897306)
XLA Ops:
  0.6 84.3 %shard_map.50 = (f32[1,1024]{1,0:T(1,128)}, f32[2,1,256]{2,1,0:T(1,128)}) custom-call(s32[2,1,256]{2,1,0:T(1,128)} %bitcast.3, bf16[512,768]{1,0:T(8,128)(2,1)} %ingest_ref.1, bf16[1024,768]{1,0:T(8,128)(2,1)} %resident_ref.1), custom_call_target="tpu_custom_call" | custom-call | tf_op jit(solution)/shard_map/pallas_call | solution.py:1076
  85.0 1.3 %shard_map.51 = (f32[1,1024]{1,0:T(1,128)}, f32[2,1,256]{2,1,0:T(1,128)}) custom-call(f32[1,1024]{1,0:T(1,128)} %get-tuple-element.6.resident_total, f32[2,1,256]{2,1,0:T(1,128)} %get-tuple-element.7.ingest_total), custom_call_target="tpu_custom_call" | custom-call | tf_op jit(solution)/shard_map/pallas_call | solution.py:429

commit v3 on v1

--- a/solution.py
+++ b/solution.py
@@ -111,6 +111,8 @@
 RESIDENT_CHUNK = 256
 HALVES = 2
 MESH = pl.DeviceIdType.MESH
+DENSE_VMEM = 55200 * 1024
+SCORE_VMEM = 1024 * 1024
 
 
 def dense_kernel(
@@ -277,6 +279,10 @@
     def _(j):
         work(line * chunks + j, 0, 1)
 
+    def gather_slot(slot):
+        block = by_resident[slot * held:(slot + 1) * held, :]
+        resident_sums[slot] = jnp.sum(block.T, axis=0, keepdims=True)
+
     def place(step):
         if not holds_back:
             return step
@@ -291,7 +297,7 @@
         late = (spot >= 1) & (spot < chunks)
         return jnp.where(at_end & (chunks > 1), jnp.where(late, spot + steps - chunks, turned), spot)
 
-    def take(step):
+    def take(step, tail=False):
         spot = place(step)
         hop, j = spot // chunks + 1, spot % chunks
 
@@ -321,6 +327,23 @@
             @pl.when((step == (line_size - 2) * chunks - 1) & below_end)
             def _():
                 start_all(down_copies(line * chunks + chunks - 1))
+
+        def near_work(first, last):
+            @pl.loop(0, 2)
+            def _(way):
+                other = line + (2 * way - 1) * hop
+
+                @pl.when((other >= 0) & (other < line_size))
+                def _():
+                    work(other * chunks + j, first, last)
+
+        if tail:
+            near_work(1, 2)
+            for slot in (3, 2):
+                gather_slot(slot)
+                part_copy(slot).start()
+            near_work(0, 1)
+            return
 
         @pl.when(step < pieces)
         def _():
@@ -367,24 +390,21 @@
     early = pieces < steps
     if early:
         return_terms(False)
-    take(steps - 1)
-    if not early:
+        take(steps - 1, tail=True)
+    else:
+        take(steps - 1)
         return_terms(False)
     return_terms(True)
     mine = pl.ds(line * chunks, chunks)
     ingest_sums[mine] = jnp.sum(by_ingest[mine], axis=1, keepdims=True)
 
-    def gather_slot(slot):
-        block = by_resident[slot * held:(slot + 1) * held, :]
-        resident_sums[slot] = jnp.sum(block.T, axis=0, keepdims=True)
-
-    gather_slot(3)
-    gather_slot(2)
-    part_copy(3).start()
+    if not early:
+        for slot in (3, 2):
+            gather_slot(slot)
+            part_copy(slot).start()
     gather_slot(1)
-    part_copy(2).start()
+    part_copy(1).start()
     gather_slot(0)
-    part_copy(1).start()
 
     for c in range(line_size * chunks):
         @pl.when((c // chunks <= line) & (line + 1 < line_size))
@@ -460,7 +480,9 @@
             dma((4,)), dma((4,)),
             dma((line_size,)), dma((line_size,)),
         ],
-        compiler_params=pltpu.CompilerParams(collective_id=0, has_side_effects=True),
+        compiler_params=pltpu.CompilerParams(
+            collective_id=0, has_side_effects=True, vmem_limit_bytes=DENSE_VMEM
+        ),
     )(cluster_ids.reshape(chunks, 1, INGEST_CHUNK), ingest, resident)
     resident_score, ingest_score = pl.pallas_call(
         score_kernel,
@@ -470,6 +492,7 @@
         ),
         in_specs=[vmem] * 2,
         out_specs=(vmem, vmem),
+        compiler_params=pltpu.CompilerParams(vmem_limit_bytes=SCORE_VMEM),
     )(resident_total, ingest_total)
     return (resident_score.reshape(held), ingest_score.reshape(count))
 

time: 65.9 us -> 64 us (0.971)
  Pallas kernels: 65.1 us -> 62.5 us
  local copies, waits for them, and re-layouts: 0 us -> 0.67 us
    pallas_call x1, Pallas kernels: 63.8 us -> 61.9 us  [dense_on_device(): pl.pallas_call(functools.partial(dense_kernel, cycle), out_shape=(jax.Sha...]
    unnamed x0 -> x2, local copies, waits for them, and re-layouts: none -> 0.67 us
    pallas_call x1, Pallas kernels: 1.28 us -> 0.6 us  [dense_on_device(): pl.pallas_call(score_kernel, out_shape=(jax.ShapeDtypeStruct(resident_tot...]
where the time goes in v3:
time: 64 us; the launch traced here: 63.8 us
  Pallas kernels  62.5 us (98%)
  local copies, waits for them, and re-layouts  0.67 us (1%)
  between operations  0.65 us (1%)
    pallas_call x1, Pallas kernels, dense_on_device(): pl.pallas_call(functools.partial(dense_kernel, cycle), out_shape=(jax.Sha...  61.9 us

profile of v3, /device:TPU:0, one launch (start us, length us, event | category | flops | bytes accessed | tf_op | source)
XLA Modules:
  0.0 63.8 jit_solution(9077948209904905518)
XLA Ops:
  0.6 0.0 copy-start
  0.6 0.7 %copy-done = s32[512]{0:T(512)S(1)} copy-done((s32[512]{0:T(512)S(1)}, s32[512]{0:T(512)}, u32[]{:S(2)}) %copy-start) | copy-done | bytes 2072
  1.3 61.9 %shard_map.50 = (f32[1,1024]{1,0:T(1,128)S(1)}, f32[2,1,256]{2,1,0:T(1,128)S(1)}) custom-call(s32[2,1,256]{2,1,0:T(1,128)S(1)} %bitcast.3, bf16[512,768]{1,0:T(8,128)(2,1)} %ingest_ref.1, bf16[1024,768]{1,0:T(8,128)(2,1)} %resident_ref.1), custom_call_target="tpu_custom_call" | custom-call | tf_op jit(solution)/shard_map/pallas_call | solution.py:454
  63.2 0.6 shard_map.51
Async XLA Ops:
  0.6 0.7 %copy-start = (s32[512]{0:T(512)S(1)}, s32[512]{0:T(512)}, u32[]{:S(2)}) copy-start(s32[512]{0:T(512)} %param.5) | copy-start | bytes 6148

commit v4 on v3

--- a/solution.py
+++ b/solution.py
@@ -201,7 +201,7 @@
         )
 
     barrier = pltpu.get_barrier_semaphore()
-    for where in (sibling, peer, across):
+    for where in (sibling, peer):
         pl.semaphore_signal(barrier, inc=1, device_id=where, device_id_type=MESH)
 
     @pl.when(line > 0)
@@ -227,7 +227,7 @@
     for j in range(chunks):
         rows[line * chunks + j] = unit(raw_ingest[j * INGEST_CHUNK:(j + 1) * INGEST_CHUNK, :])
     ids_load.wait()
-    pl.semaphore_wait(barrier, 3 + (line > 0).astype(jnp.int32) + (line + 1 < line_size).astype(jnp.int32))
+    pl.semaphore_wait(barrier, 2 + (line > 0).astype(jnp.int32) + (line + 1 < line_size).astype(jnp.int32))
     for j in range(chunks):
         kept = holds_back and j == chunks - 1
 

time: 64 us -> 63.9 us (level)
  no operation moved by 1% of the time
where the time goes in v4:
time: 63.9 us; the launch traced here: 63.8 us
  Pallas kernels  62.4 us (98%)
  local copies, waits for them, and re-layouts  0.67 us (1%)
  between operations  0.65 us (1%)
    pallas_call x1, Pallas kernels, dense_on_device(): pl.pallas_call(functools.partial(dense_kernel, cycle), out_shape=(jax.Sha...  61.8 us

profile of v4, /device:TPU:0, one launch (start us, length us, event | category | flops | bytes accessed | tf_op | source)
XLA Modules:
  0.0 63.8 jit_solution(10384327561989536451)
XLA Ops:
  0.6 0.0 copy-start
  0.6 0.7 %copy-done = s32[512]{0:T(512)S(1)} copy-done((s32[512]{0:T(512)S(1)}, s32[512]{0:T(512)}, u32[]{:S(2)}) %copy-start) | copy-done | bytes 2072
  1.3 61.8 %shard_map.50 = (f32[1,1024]{1,0:T(1,128)S(1)}, f32[2,1,256]{2,1,0:T(1,128)S(1)}) custom-call(s32[2,1,256]{2,1,0:T(1,128)S(1)} %bitcast.3, bf16[512,768]{1,0:T(8,128)(2,1)} %ingest_ref.1, bf16[1024,768]{1,0:T(8,128)(2,1)} %resident_ref.1), custom_call_target="tpu_custom_call" | custom-call | tf_op jit(solution)/shard_map/pallas_call | solution.py:454
  63.2 0.6 shard_map.51
Async XLA Ops:
  0.6 0.7 %copy-start = (s32[512]{0:T(512)S(1)}, s32[512]{0:T(512)}, u32[]{:S(2)}) copy-start(s32[512]{0:T(512)} %param.5) | copy-start | bytes 6148
